TPU v7x, 128 devices: a whole 4x4x4 slice. The times are simulated.
128 devices in a mesh: rows: 32 (over y, x, core), model: 4 (over z).
Axes of the slice: x: 4, y: 4, z: 4, core: 2. Of those that a mesh axis runs over, the one named last changes fastest.
Arguments:
- weight_gate: bfloat16 [2048, 8192], P('rows', 'model'), may hold values from -0.125 to 0.125
- low_gate: bfloat16 [2048, 64], P('rows'), may hold values from -0.125 to 0.125
- high_gate: bfloat16 [64, 8192], P(None, 'model'), may hold values from -0.75 to 0.75
- weight_up: bfloat16 [2048, 8192], P('rows', 'model'), may hold values from -0.125 to 0.125
- low_up: bfloat16 [2048, 64], P('rows'), may hold values from -0.125 to 0.125
- high_up: bfloat16 [64, 8192], P(None, 'model'), may hold values from -0.75 to 0.75
- weight_down: bfloat16 [8192, 2048], P('model', 'rows'), may hold values from -0.0625 to 0.0625
- low_down: bfloat16 [8192, 64], P('model'), may hold values from -0.0625 to 0.0625
- high_down: bfloat16 [64, 2048], P(None, 'rows'), may hold values from -0.75 to 0.75
- norm_train: float32 [2048], P(('rows', 'model')), may hold values from 0.25 to 1.75
- norm_step: float32 [2048], P(('rows', 'model')), may hold values from -0.3 to 0.3
Outputs:
- final_gate: bfloat16 [8192, 2048], P('model')
- final_up: bfloat16 [8192, 2048], P('model')
- final_down: bfloat16 [2048, 8192], P(None, 'model')
- serve_norm: bfloat16 [2048], replicated
All inputs are finite; a program needn't handle non-finite values.
Results may differ from a plain program's by a relative error of at most 0.001.
Values may be sent and summed in bfloat16 or wider, within the bound.
A program may use at most 192 MiB of HBM per device.

v0:
```python
import jax
import jax.numpy as jnp
from jax import lax
from jax.sharding import Mesh
from jax.sharding import PartitionSpec as P

ROWS = ("rows_0", "rows_1", "rows_2")
ROWS_MODEL = ("rows_0", "rows_1", "rows_2", "model")
mix_rate = 0.5


def turned_gather(arrays, axis, dims):
    turned = [jnp.moveaxis(a, dim, 0) for a, dim in zip(arrays, dims)]
    both = jnp.concatenate([t.reshape(len(t), -1) for t in turned], axis=1)
    result, at, finished = (lax.all_gather(both, axis, axis=0, tiled=True), 0, [])
    for t, dim in zip(turned, dims):
        section = result[:, at : at + t[0].size].reshape(-1, *t.shape[1:])
        finished.append(jnp.moveaxis(section, 0, dim))
        at += t[0].size
    return tuple(finished)


def in_order(tiles, dim):
    dims = list(tiles.shape[1:])
    dims[dim] *= tiles.shape[0]
    return jnp.moveaxis(tiles, 0, dim).reshape(dims)


def stacked_from(array, axes, turns):
    tiles = array
    for k in turns:
        tiles = lax.all_gather(tiles, axes[k])
    done = turns[::-1]
    back = [done.index(k) for k in range(len(axes))]
    tiles = tiles.transpose(*back, *range(len(axes), tiles.ndim))
    return tiles.reshape(-1, *array.shape)


def gathered_by_axis(array, axes, turns, dim):
    return in_order(stacked_from(array, axes, turns), dim)


def local(
    weight_gate,
    low_gate,
    high_gate,
    weight_up,
    low_up,
    high_up,
    weight_down,
    low_down,
    high_down,
    norm_train,
    norm_step,
):
    result_gate = weight_gate.astype(jnp.float32) + mix_rate * jnp.dot(
        low_gate, high_gate, preferred_element_type=jnp.float32
    )
    result_up = weight_up.astype(jnp.float32) + mix_rate * jnp.dot(
        low_up, high_up, preferred_element_type=jnp.float32
    )
    result_down = weight_down.astype(jnp.float32) + mix_rate * jnp.dot(
        low_down, high_down, preferred_element_type=jnp.float32
    )
    narrow_gate, narrow_up, narrow_down = (
        result_gate.astype(jnp.bfloat16),
        result_up.astype(jnp.bfloat16),
        result_down.astype(jnp.bfloat16),
    )
    final_gate, final_up, final_down = turned_gather(
        (narrow_gate, narrow_up, narrow_down), ROWS, (0, 0, 1)
    )
    final_gate, final_up, final_down = (final_gate.T, final_up.T, final_down.T)
    serve_norm = gathered_by_axis(
        (norm_train + norm_step).astype(jnp.bfloat16), ROWS_MODEL, (0, 1, 3, 2), 0
    )
    return (final_gate, final_up, final_down, serve_norm)


def solution(mesh):
    split = Mesh(
        mesh.devices.reshape(4, 4, 2, mesh.shape["model"]), ("rows_0", "rows_1", "rows_2", "model")
    )
    placed = (
        P(ROWS, "model"),
        P(ROWS, None),
        P(None, "model"),
        P(ROWS, "model"),
        P(ROWS, None),
        P(None, "model"),
        P("model", ROWS),
        P("model", None),
        P(None, ROWS),
        P(ROWS_MODEL),
        P(ROWS_MODEL),
    )
    return jax.shard_map(
        local,
        mesh=split,
        in_specs=placed,
        out_specs=(P("model", None), P("model", None), P(None, "model"), P()),
        check_vma=False,
    )
```

profile of v0, /device:TPU:1, one launch (start us, length us, event | category | flops | bytes accessed | tf_op | source)
XLA Modules:
  0.0 156.6 jit_solution(8086940729364175655)
XLA Ops:
  7.2 0.0 copy-start
  7.2 0.0 all-gather.7.cloned.1.call-start
  7.2 0.9 copy-done
  8.1 1.2 fusion.4
  9.3 1.3 fusion.5
  10.6 1.3 fusion.6
  11.9 0.9 pad_maximum_fusion
  12.8 0.0 all-gather.7.cloned.1.call-update
  12.9 1.2 dynamic-slice
  14.8 0.7 add_convert_fusion
  15.4 0.2 dynamic-update-slice
  15.6 9.5 %all-reduce = bf16[64]{0:T(256)(128)(2,1)S(1)} all-reduce(bf16[64]{0:T(256)(128)(2,1)S(1)} %dynamic-update-slice), channel_id=2, replica_groups=mesh['rows_0'=4,'rows_1'=4,'rows_2'=2,'model'=4] {'rows_0'}, use_global_device_ids=true, to_apply=%add | all-reduce | flops 64 | bytes 256
  25.2 0.1 reshape.15
  25.2 8.7 %all-gather.4 = bf16[4,4,16]{2,1,0:T(4,128)(2,1)S(1)} all-gather(bf16[1,4,16]{2,1,0:T(4,128)(2,1)S(1)} %reshape.15), channel_id=3, replica_groups=mesh['rows_0'=4,'rows_1'=4,'rows_2'=2,'model'=4] {'rows_1'}, dimensions={0}, use_global_device_ids=true | all-gather | bytes 640 | tf_op jit(solution)/shard_map/all_gather | solution.py:32
  33.9 11.1 %all-gather.2 = bf16[16,4,16]{2,1,0:T(4,128)(2,1)S(1)} all-gather(bf16[4,4,16]{2,1,0:T(4,128)(2,1)S(1)} %all-gather.4), channel_id=4, replica_groups=mesh['rows_0'=4,'rows_1'=4,'rows_2'=2,'model'=4] {'model'}, dimensions={0}, use_global_device_ids=true | all-gather | bytes 2560 | tf_op jit(solution)/shard_map/all_gather | solution.py:32
  45.0 7.4 %all-gather.3 = bf16[8,4,4,16]{3,2,1,0:T(4,128)(2,1)S(1)} all-gather(bf16[4,4,4,16]{3,2,1,0:T(4,128)(2,1)S(1)} %bitcast.20), channel_id=5, replica_groups=mesh['rows_0'=4,'rows_1'=4,'rows_2'=2,'model'=4] {'rows_2'}, dimensions={0}, use_global_device_ids=true | all-gather | bytes 6144 | tf_op jit(solution)/shard_map/all_gather | solution.py:32
  52.4 0.7 reshape_reshape.3
  53.1 55.3 %all-gather.7.cloned.1.call-done = bf16[2048,6144]{1,0:T(8,128)(2,1)} async-done(((bf16[64,6144]{1,0:T(8,128)(2,1)}), bf16[2048,6144]{1,0:T(8,128)(2,1)}) %all-gather.7.cloned.1.call-update) | async-done | bytes 25165840 | tf_op jit(solution)/shard_map/all_gather | solution.py:15
  108.4 16.9 %fusion.7 = (bf16[2048,2048]{1,0:T(8,128)(2,1)}, bf16[2048,2048]{0,1:T(8,128)(2,1)}, bf16[2048,2048]{0,1:T(8,128)(2,1)}) fusion(bf16[2048,6144]{1,0:T(8,128)(2,1)} %all-gather.7.cloned.1.call-done), kind=kLoop, calls=%fused_computation.15 | loop fusion | bytes 50331648 | tf_op jit(solution)/shard_map/slice | solution.py:17
  125.3 12.2 %copy.21 = bf16[2048,2048]{1,0:T(8,128)(2,1)} copy(bf16[2048,2048]{0,1:T(8,128)(2,1)} %get-tuple-element.18) | data formatting | bytes 16777216
  137.5 0.0 copy-start.1
  137.5 12.3 %copy.22 = bf16[2048,2048]{1,0:T(8,128)(2,1)} copy(bf16[2048,2048]{0,1:T(8,128)(2,1)} %get-tuple-element.17) | data formatting | bytes 16777216
  149.8 0.0 copy-done.1
  (2 shorter events, 0.0 us)
Async XLA Ops:
  7.2 1.0 copy-start
  7.2 101.2 %all-gather.7.cloned.1.call-start = ((), (), s32[]{:S(2)}) async-start(), calls=%async_computation | async-start | bytes 25952256 | tf_op jit(solution)/shard_map/all_gather | solution.py:15
  137.5 12.3 %copy-start.1 = (bf16[64,2048]{1,0:T(8,128)(2,1)S(1)}, bf16[64,2048]{1,0:T(8,128)(2,1)}, u32[]{:S(2)}) copy-start(bf16[64,2048]{1,0:T(8,128)(2,1)} %param.16) | copy-start | bytes 786436
Sparse Core Ops, SparseCore 0:
  13.0 95.3 all-gather.6
where the time goes:
time: 157 us
  waiting for transfers between devices  55.3 us (35%)
  local copies, waits for them, and re-layouts  44.6 us (28%)
  blocking collectives  36.6 us (23%)
  between operations  14.7 us (9%)
  matrix products  3.75 us (2%)
  other arithmetic  1.61 us (1%)
    all_gather x1, waiting for transfers between devices, turned_gather(): lax.all_gather(both, axis, axis=0, tiled=True)  55.3 us
    all_gather x3, blocking collectives, stacked_from(): tiles = lax.all_gather(tiles, axes[k])  27.1 us
    unnamed x10, local copies, waits for them, and re-layouts  26.9 us
    slice x1, local copies, waits for them, and re-layouts, turned_gather(): section = result[:, at:at + t[0].size].reshape(-1, *t.shape[1:])  16.9 us
    unnamed x1, blocking collectives  9.52 us
  transfers between devices with their start and end apart: 1, of which 1 were waited for; matrix products, arithmetic and copies ran while one was open for 2% of the time, Pallas kernels for 0%

commit v1 on v0

--- a/solution.py
+++ b/solution.py
@@ -9,10 +9,17 @@
 mix_rate = 0.5
 
 
+def gather_over(x, axis, d):
+    size = lax.axis_size(axis)
+    blocks = jnp.stack([x for _ in range(size)])
+    blocks = lax.all_to_all(blocks, axis, split_axis=0, concat_axis=0)
+    return jnp.concatenate(blocks, axis=d)
+
+
 def turned_gather(arrays, axis, dims):
     turned = [jnp.moveaxis(a, dim, 0) for a, dim in zip(arrays, dims)]
     both = jnp.concatenate([t.reshape(len(t), -1) for t in turned], axis=1)
-    result, at, finished = (lax.all_gather(both, axis, axis=0, tiled=True), 0, [])
+    result, at, finished = (gather_over(both, axis, 0), 0, [])
     for t, dim in zip(turned, dims):
         section = result[:, at : at + t[0].size].reshape(-1, *t.shape[1:])
         finished.append(jnp.moveaxis(section, 0, dim))

time: 157 us -> 402 us (2.56); the launches traced: 157 us -> 397 us
  blocking collectives: 36.6 us -> 331 us
  waiting for transfers between devices: 55.3 us -> 0.01 us
  between operations: 14.7 us -> 1.37 us
  starting transfers between devices: 0.04 us -> 8.76 us
  local copies, waits for them, and re-layouts: 44.6 us -> 52.6 us
    unnamed x1, blocking collectives: 9.52 us -> 298 us
    all_gather x1 -> x0, waiting for transfers between devices: 55.3 us -> none  [turned_gather(): lax.all_gather(both, axis, axis=0, tiled=True)]
    all_to_all x0 -> x1, starting transfers between devices: none -> 8.76 us  [gather_over(): blocks = lax.all_to_all(blocks, axis, split_axis=0, concat_axis=0)]
    another operation x0 -> x1, local copies, waits for them, and re-layouts: none -> 8.65 us  [gather_over(): blocks = jnp.stack([x for _ in range(size)])]
    all_gather x3, blocking collectives: 27.1 us -> 32.4 us  [stacked_from(): tiles = lax.all_gather(tiles, axes[k])]
    unnamed x10 -> x16, local copies, waits for them, and re-layouts: 26.9 us -> 26.4 us
  transfers between devices with their start and end apart: 1 -> 1, of which waited for: 1 -> 0; matrix products, arithmetic and copies ran while one was open for 2% -> 0% of each run, Pallas kernels for 0% -> 0%
where the time goes in v1:
time: 402 us; the launch traced here: 397 us
  blocking collectives  331 us (82%)
  local copies, waits for them, and re-layouts  52.6 us (13%)
  starting transfers between devices  8.76 us (2%)
    unnamed x1, blocking collectives  298 us
    all_gather x3, blocking collectives, stacked_from(): tiles = lax.all_gather(tiles, axes[k])  32.4 us
    unnamed x16, local copies, waits for them, and re-layouts  26.4 us
    slice x1, local copies, waits for them, and re-layouts, turned_gather(): section = result[:, at:at + t[0].size].reshape(-1, *t.shape[1:])  16.9 us
    all_to_all x1, starting transfers between devices, gather_over(): blocks = lax.all_to_all(blocks, axis, split_axis=0, concat_axis=0)  8.76 us
    another operation x1, local copies, waits for them, and re-layouts, gather_over(): blocks = jnp.stack([x for _ in range(size)])  8.65 us
  transfers between devices with their start and end apart: 1, of which 0 were waited for; matrix products, arithmetic and copies ran while one was open for 0% of the time, Pallas kernels for 0%

profile of v1, /device:TPU:1, one launch (start us, length us, event | category | flops | bytes accessed | tf_op | source)
XLA Modules:
  0.0 397.3 jit_solution(5101727194362285379)
XLA Ops:
  0.6 0.0 copy-start
  0.6 0.9 copy-done
  1.6 1.2 fusion.4
  2.8 1.3 fusion.5
  4.0 1.3 fusion.6
  5.4 0.1 pad_maximum_fusion
  5.4 8.6 %stack.2 = bf16[32,64,6144]{2,1,0:T(8,128)(2,1)} broadcast(bf16[64,6144]{1,0:T(8,128)(2,1)S(1)} %pad_maximum_fusion), dimensions={1,2} | broadcast | bytes 25952256 | tf_op jit(solution)/shard_map/stack | solution.py:14
  14.1 0.0 copy-start.4
  14.1 0.0 copy-start.2
  14.1 0.0 copy-start.3
  14.1 8.8 %all-to-all-start = ((bf16[32,64,6144]{2,1,0:T(8,128)(2,1)}), bf16[32,64,6144]{2,1,0:T(8,128)(2,1)}, u32[]{:S(2)}, u32[]{:S(2)}) async-start(bf16[32,64,6144]{2,1,0:T(8,128)(2,1)} %stack.2), calls=%async_computation | async-start | bytes 50331648 | tf_op jit(solution)/shard_map/all_to_all | solution.py:15
  22.8 0.0 copy-done.4
  22.9 0.6 dynamic-slice
  24.1 0.0 copy-done.2
  24.1 0.0 copy-done.3
  24.1 0.2 dynamic-update-slice
  24.4 298.3 %all-reduce = bf16[64]{0:T(256)(128)(2,1)S(1)} all-reduce(bf16[64]{0:T(256)(128)(2,1)S(1)} %dynamic-update-slice), channel_id=2, replica_groups=mesh['rows_0'=4,'rows_1'=4,'rows_2'=2,'model'=4] {'rows_0'}, use_global_device_ids=true, to_apply=%add | all-reduce | flops 64 | bytes 256
  322.7 0.1 reshape.21
  322.8 16.3 %all-gather.4 = bf16[4,4,16]{2,1,0:T(4,128)(2,1)S(1)} all-gather(bf16[1,4,16]{2,1,0:T(4,128)(2,1)S(1)} %reshape.21), channel_id=3, replica_groups=mesh['rows_0'=4,'rows_1'=4,'rows_2'=2,'model'=4] {'rows_1'}, dimensions={0}, use_global_device_ids=true | all-gather | bytes 640 | tf_op jit(solution)/shard_map/all_gather | solution.py:39
  339.1 10.3 %all-gather.2 = bf16[16,4,16]{2,1,0:T(4,128)(2,1)S(1)} all-gather(bf16[4,4,16]{2,1,0:T(4,128)(2,1)S(1)} %all-gather.4), channel_id=4, replica_groups=mesh['rows_0'=4,'rows_1'=4,'rows_2'=2,'model'=4] {'model'}, dimensions={0}, use_global_device_ids=true | all-gather | bytes 2560 | tf_op jit(solution)/shard_map/all_gather | solution.py:39
  349.4 5.8 %all-gather.3 = bf16[8,4,4,16]{3,2,1,0:T(4,128)(2,1)S(1)} all-gather(bf16[4,4,4,16]{3,2,1,0:T(4,128)(2,1)S(1)} %bitcast.21), channel_id=5, replica_groups=mesh['rows_0'=4,'rows_1'=4,'rows_2'=2,'model'=4] {'rows_2'}, dimensions={0}, use_global_device_ids=true | all-gather | bytes 6144 | tf_op jit(solution)/shard_map/all_gather | solution.py:39
  355.2 0.7 reshape_reshape.3
  355.9 0.0 all-to-all-done
  355.9 16.9 %fusion.7 = (bf16[2048,2048]{1,0:T(8,128)(2,1)}, bf16[2048,2048]{0,1:T(8,128)(2,1)}, bf16[2048,2048]{0,1:T(8,128)(2,1)}) fusion(bf16[2048,6144]{1,0:T(8,128)(2,1)} %bitcast.1), kind=kLoop, calls=%fused_computation.15 | loop fusion | bytes 50331648 | tf_op jit(solution)/shard_map/slice | solution.py:24
  372.8 12.2 %copy.21 = bf16[2048,2048]{1,0:T(8,128)(2,1)} copy(bf16[2048,2048]{0,1:T(8,128)(2,1)} %get-tuple-element.18) | data formatting | bytes 16777216
  385.1 0.0 copy-start.1
  385.1 12.3 %copy.22 = bf16[2048,2048]{1,0:T(8,128)(2,1)} copy(bf16[2048,2048]{0,1:T(8,128)(2,1)} %get-tuple-element.17) | data formatting | bytes 16777216
  397.3 0.0 copy-done.1
  (3 shorter events, 0.0 us)
Async XLA Ops:
  0.6 1.0 copy-start
  14.1 8.8 %copy-start.4 = (u32[128]{0:T(128)S(1)}, u32[128]{0:T(128)}, u32[]{:S(2)}) copy-start(u32[128]{0:T(128)} %constant.7) | copy-start | bytes 1540
  14.1 10.0 %copy-start.2 = (f32[16]{0:T(128)S(1)}, f32[16]{0:T(128)}, u32[]{:S(2)}) copy-start(f32[16]{0:T(128)} %param.20) | copy-start | bytes 196
  14.1 10.0 %copy-start.3 = (f32[16]{0:T(128)S(1)}, f32[16]{0:T(128)}, u32[]{:S(2)}) copy-start(f32[16]{0:T(128)} %param.21) | copy-start | bytes 196
  14.1 341.9 %all-to-all-start = ((bf16[32,64,6144]{2,1,0:T(8,128)(2,1)}), bf16[32,64,6144]{2,1,0:T(8,128)(2,1)}, u32[]{:S(2)}, u32[]{:S(2)}) async-start(bf16[32,64,6144]{2,1,0:T(8,128)(2,1)} %stack.2), calls=%async_computation | async-start | bytes 50331648 | tf_op jit(solution)/shard_map/all_to_all | solution.py:15
  385.1 12.3 %copy-start.1 = (bf16[64,2048]{1,0:T(8,128)(2,1)S(1)}, bf16[64,2048]{1,0:T(8,128)(2,1)}, u32[]{:S(2)}) copy-start(bf16[64,2048]{1,0:T(8,128)(2,1)} %param.16) | copy-start | bytes 786436
